TPU v7x, 32 devices: a whole 2x2x4 slice. The times are simulated.
32 devices in a mesh: parts: 2 (over y), blk: 4 (over x, core), sub: 4 (over z).
Axes of the slice: x: 2, y: 2, z: 4, core: 2. Of those that a mesh axis runs over, the one named last changes fastest.
Arguments:
- tokens: bfloat16 [256, 4096], P(('parts', 'blk'), 'sub'), parts along dimension 0, may hold values from -6 to 6
- expert_ids: int32 [256, 2], P(('parts', 'blk')), parts along dimension 0, may hold values from 0 to 7, all different within a row; in each aligned block of 32 rows (0 to 31, 32 to 63, ...) at most 16 rows name the same one
- gate_level: int32 [256, 2], P(('parts', 'blk')), parts along dimension 0, may hold values from 0 to 15
- gate_weight: bfloat16 [8, 4096, 8192], P('blk', None, 'sub'), may hold values from -0.09375 to 0.09375
- up_weight: bfloat16 [8, 4096, 8192], P('blk', None, 'sub'), may hold values from -0.09375 to 0.09375
- down_weight: bfloat16 [8, 8192, 4096], P('blk', 'sub'), may hold values from -0.0625 to 0.0625
Outputs:
- mixed_out: bfloat16 [256, 4096], P(('parts', 'blk'), 'sub'), parts along dimension 0
There are 2 independent parts, one for each index of `parts`. A program takes and returns all parts, laid end to end along the dimension named above; an argument that names none is the same for every part. Nothing has to cross between parts.
Inputs may be any that keep to these rules, and one draw needn't show every extreme that they name: `expert_ids`: A token's 2 experts differ. Among the 32 tokens of one index of blk (aligned blocks of tokens), no expert is picked by more than 16 tokens, and in some block some expert is picked by exactly 16.
All inputs are finite; a program needn't handle non-finite values.
Results may differ from a plain program's by a relative error of at most 0.015.
Values may be sent and summed in bfloat16 or wider, within the bound.
A program may use at most 192 MiB of HBM per device.

v0:
```python
import jax
import jax.numpy as jnp
from jax import lax
from jax.sharding import PartitionSpec as P

E = 8
TOP = 2
CAP = 16


def shards(tokens, expert_ids, gate_level, gate_weight, up_weight, down_weight):
    block_count = lax.axis_size("blk")
    sub_count = lax.axis_size("sub")
    local_slots = gate_weight.shape[0]
    hidden_width = gate_weight.shape[2]
    slot_count = local_slots * block_count
    halves = slot_count // E
    token_rows = tokens.shape[0]
    feature_width = tokens.shape[1]
    buffer_width = slot_count * CAP
    received_rows = block_count * CAP
    picked = expert_ids.reshape(-1)
    onehot = (picked[:, None] == jnp.arange(E, dtype=jnp.int32)[None, :]).astype(jnp.int32)
    ranking = jnp.sum((jnp.cumsum(onehot, axis=0) - onehot) * onehot, axis=1)
    columns = (
        picked[:, None] * CAP
        + (jnp.arange(halves, dtype=jnp.int32) * E)[None, :] * CAP
        + ranking[:, None]
    )
    columns = columns.reshape(token_rows, TOP * halves)
    matches = columns[:, :, None] == jnp.arange(buffer_width, dtype=jnp.int32)[None, None, :]
    levels = gate_level.astype(jnp.float32) + 1.0
    shares = levels / jnp.sum(levels, axis=1, keepdims=True)
    shares_wide = jnp.repeat(shares, halves, axis=1)
    combine_weights = jnp.sum(matches.astype(jnp.float32) * shares_wide[:, :, None], axis=1)
    chosen = jnp.any(matches, axis=1).astype(jnp.bfloat16)
    outgoing = lax.dot_general(
        chosen, tokens, (((0,), (0,)), ((), ())), preferred_element_type=jnp.float32
    )
    outgoing = outgoing.astype(jnp.bfloat16).reshape(slot_count, CAP, feature_width)
    copies = jnp.broadcast_to(
        outgoing.reshape(block_count, 1, local_slots, CAP, feature_width),
        (block_count, sub_count, local_slots, CAP, feature_width),
    )
    copies = copies.reshape(block_count * sub_count, local_slots, CAP, feature_width)
    arrived = lax.all_to_all(copies, ("blk", "sub"), split_axis=0, concat_axis=0, tiled=True)
    arrived = arrived.reshape(block_count, sub_count, local_slots, CAP, feature_width)
    gate_split = gate_weight.reshape(local_slots, sub_count, feature_width, hidden_width)
    up_split = up_weight.reshape(local_slots, sub_count, feature_width, hidden_width)
    gate_acts = jnp.einsum(
        "bsncd,nsdf->nbcf", arrived, gate_split, preferred_element_type=jnp.float32
    )
    up_acts = jnp.einsum("bsncd,nsdf->nbcf", arrived, up_split, preferred_element_type=jnp.float32)
    gate_acts = gate_acts.reshape(local_slots, received_rows, hidden_width)
    up_acts = up_acts.reshape(local_slots, received_rows, hidden_width)
    hidden = (jax.nn.silu(gate_acts) * up_acts).astype(jnp.bfloat16)
    full_out = jnp.einsum("nrf,nfd->nrd", hidden, down_weight, preferred_element_type=jnp.float32)
    local_out = lax.psum_scatter(
        full_out.astype(jnp.bfloat16), "sub", scatter_dimension=2, tiled=True
    )
    home_rows = lax.all_to_all(local_out, "blk", split_axis=1, concat_axis=0, tiled=True)
    home_flat = home_rows.reshape(buffer_width, feature_width).astype(jnp.float32)
    mixed_out = jnp.dot(
        combine_weights,
        home_flat,
        precision=lax.Precision.HIGHEST,
        preferred_element_type=jnp.float32,
    )
    return mixed_out.astype(jnp.bfloat16)


def solution(mesh):
    return jax.shard_map(
        shards,
        mesh=mesh,
        in_specs=(
            P(("parts", "blk"), "sub"),
            P(("parts", "blk"), None),
            P(("parts", "blk"), None),
            P("blk", None, "sub"),
            P("blk", None, "sub"),
            P("blk", "sub", None),
        ),
        out_specs=P(("parts", "blk"), "sub"),
        check_vma=False,
    )
```

profile of v0, /device:TPU:0, one launch (start us, length us, event | category | flops | bytes accessed | tf_op | source)
XLA Modules:
  0.0 130.9 jit_solution(14647058199489605425)
XLA Ops:
  6.5 0.0 copy-start
  6.5 0.0 reduce-scatter.2.cloned.1.call-start
  6.5 0.8 copy.40
  7.3 0.1 eq.28
  7.4 0.1 fusion.5
  7.5 0.1 reduce_window_sum.11
  7.6 0.2 select_reduce_fusion.1
  7.8 0.1 reduce_sum.30
  7.9 0.1 copy.41
  8.0 0.7 multiply_add_fusion
  8.7 0.1 fusion.4
  8.8 0.0 copy-done
  8.8 0.3 convolution_convert_fusion.1
  9.0 0.1 broadcast_in_dim.5
  9.2 34.0 %all_to_all.20 = bf16[16,2,16,1024]{3,2,1,0:T(8,128)(2,1)S(1)} all-to-all(bf16[16,2,16,1024]{3,2,1,0:T(8,128)(2,1)S(1)} %bitcast.54), channel_id=1, replica_groups=mesh['parts'=2,'blk'=4,'sub'=4] {'blk','sub'}, dimensions={0} | all-to-all | bytes 2097152 | tf_op jit(solution)/shard_map/all_to_all | solution.py:46
  43.2 0.1 copy.42
  43.3 13.6 %fusion.8 = f32[2,4,16,2048,1]{3,2,4,1,0:T(8,128)S(1)} fusion(bf16[4,4,2,16,1024]{4,3,1,0,2:T(8,128)(2,1)S(1)} %bitcast.52, bf16[2,4,1024,2048,1]{3,2,1,4,0:T(8,128)(2,1)} %bitcast.50), kind=kOutput, calls=%fused_computation.20 | convolution fusion | flops 2147483648 | bytes 35651584 | tf_op jit(solution)/shard_map/bsncd,nsdf->nbcf/dot_general | solution.py:50
  56.9 0.0 copy-start.1
  56.9 13.6 %fusion.9 = f32[2,4,16,2048,1]{3,2,4,1,0:T(8,128)S(1)} fusion(bf16[4,4,2,16,1024]{4,3,1,0,2:T(8,128)(2,1)S(1)} %bitcast.53, bf16[2,4,1024,2048,1]{3,2,1,4,0:T(8,128)(2,1)} %bitcast.51), kind=kOutput, calls=%fused_computation.21 | convolution fusion | flops 2147483648 | bytes 35651584 | tf_op jit(solution)/shard_map/bsncd,nsdf->nbcf/dot_general | solution.py:53
  70.6 0.3 fusion
  70.9 14.7 %convolution_convert_fusion = bf16[2,64,4096]{2,1,0:T(8,128)(2,1)} fusion(bf16[2,64,2048]{2,1,0:T(8,128)(2,1)S(1)} %fusion, bf16[2,2048,4096]{2,1,0:T(8,128)(2,1)} %param.11), kind=kOutput, calls=%fused_computation | convolution fusion | flops 2148007936 | bytes 35127296 | tf_op jit(solution)/shard_map/nrf,nfd->nrd/dot_general | solution.py:57
  85.5 0.0 reduce-scatter.2.cloned.1.call-update
  85.6 0.0 copy-done.1
  85.6 26.2 %reduce-scatter.2.cloned.1.call-done = bf16[2,64,1024]{2,1,0:T(8,128)(2,1)} async-done(((bf16[2,64,4096]{2,1,0:T(8,128)(2,1)}), bf16[2,64,1024]{2,1,0:T(8,128)(2,1)}) %reduce-scatter.2.cloned.1.call-update) | async-done | bytes 262160 | tf_op jit(solution)/shard_map/reduce_scatter | solution.py:58
  111.8 1.9 %copy.43 = bf16[2,64,1024]{2,0,1:T(2,128)(2,1)} copy(bf16[2,64,1024]{2,1,0:T(8,128)(2,1)} %reduce-scatter.2.cloned.1.call-done) | data formatting | bytes 524288 | tf_op jit(solution)/shard_map/reduce_scatter | solution.py:58
  113.7 3.4 %all-to-all-start.1 = ((bf16[2,64,1024]{2,0,1:T(2,128)(2,1)}), bf16[2,64,1024]{2,0,1:T(2,128)(2,1)S(1)}, u32[]{:S(2)}, u32[]{:S(2)}) async-start(bf16[2,64,1024]{2,0,1:T(2,128)(2,1)} %copy.43), calls=%async_computation.2 | async-start | bytes 524288 | tf_op jit(solution)/shard_map/all_to_all | solution.py:61
  117.1 0.1 select_reduce_fusion
  117.2 5.9 %all-to-all-done.1 = bf16[2,64,1024]{2,0,1:T(2,128)(2,1)S(1)} async-done(((bf16[2,64,1024]{2,0,1:T(2,128)(2,1)}), bf16[2,64,1024]{2,0,1:T(2,128)(2,1)S(1)}, u32[]{:S(2)}, u32[]{:S(2)}) %all-to-all-start.1) | async-done | bytes 262176 | tf_op jit(solution)/shard_map/all_to_all | solution.py:61
  123.1 0.9 convolution_convert_fusion.2
  (4 shorter events, 0.1 us)
Async XLA Ops:
  6.5 2.2 %copy-start = (bf16[32,1024]{1,0:T(8,128)(2,1)S(1)}, bf16[32,1024]{1,0:T(8,128)(2,1)}, u32[]{:S(2)}) copy-start(bf16[32,1024]{1,0:T(8,128)(2,1)} %param.6) | copy-start | bytes 196612
  6.5 105.2 %reduce-scatter.2.cloned.1.call-start = ((), (), s32[]{:S(2)}) async-start(), calls=%async_computation.3 | async-start | bytes 1310720 | tf_op jit(solution)/shard_map/reduce_scatter | solution.py:58
  56.9 28.6 %copy-start.1 = (s32[32,2]{0,1:T(2,128)S(1)}, s32[32,2]{0,1:T(2,128)}, u32[]{:S(2)}) copy-start(s32[32,2]{0,1:T(2,128)} %param.8) | copy-start | bytes 772
  113.7 9.4 %all-to-all-start.1 = ((bf16[2,64,1024]{2,0,1:T(2,128)(2,1)}), bf16[2,64,1024]{2,0,1:T(2,128)(2,1)S(1)}, u32[]{:S(2)}, u32[]{:S(2)}) async-start(bf16[2,64,1024]{2,0,1:T(2,128)(2,1)} %copy.43), calls=%async_computation.2 | async-start | bytes 524288 | tf_op jit(solution)/shard_map/all_to_all | solution.py:61
Sparse Core Ops, SparseCore 0:
  85.7 26.0 reduce-scatter.1
where the time goes:
time: 131 us
  matrix products  43 us (33%)
  blocking collectives  34 us (26%)
  waiting for transfers between devices  32.1 us (25%)
  between operations  13.5 us (10%)
  starting transfers between devices  3.41 us (3%)
  local copies, waits for them, and re-layouts  3.28 us (3%)
  other arithmetic  1.52 us (1%)
    all_to_all x1, blocking collectives, shards(): lax.all_to_all(copies, ('blk', 'sub'), split_axis=0, concat_axis=0, tiled...  34 us
    reduce_scatter x1, waiting for transfers between devices, shards(): lax.psum_scatter(full_out.astype(jnp.bfloat16), 'sub', scatter_dimension=...  26.2 us
    dot_general x1, matrix products, shards(): jnp.einsum('nrf,nfd->nrd', hidden, down_weight, preferred_element_type=jn...  14.7 us
    dot_general x1, matrix products, shards(): jnp.einsum('bsncd,nsdf->nbcf', arrived, up_split, preferred_element_type=...  13.6 us
    dot_general x1, matrix products, shards(): jnp.einsum('bsncd,nsdf->nbcf', arrived, gate_split, preferred_element_typ...  13.6 us
    all_to_all x1, waiting for transfers between devices, shards(): lax.all_to_all(local_out, 'blk', split_axis=1, concat_axis=0, tiled=True)  5.87 us
    all_to_all x1, starting transfers between devices, shards(): lax.all_to_all(local_out, 'blk', split_axis=1, concat_axis=0, tiled=True)  3.4 us
  transfers between devices with their start and end apart: 2, of which 2 were waited for; matrix products, arithmetic and copies ran while one was open for 0% of the time, Pallas kernels for 0%

commit v1 on v0

--- a/solution.py
+++ b/solution.py
@@ -1,11 +1,20 @@
+import functools
+
 import jax
 import jax.numpy as jnp
 from jax import lax
 from jax.sharding import PartitionSpec as P
 
+from jax.experimental import pallas as pl
+from jax.experimental.pallas import tpu as pltpu
+
 E = 8
 TOP = 2
 CAP = 16
+BF16 = jnp.bfloat16
+F32 = jnp.float32
+TILE = 512
+AHEAD = 6
 
 
 def shards(tokens, expert_ids, gate_level, gate_weight, up_weight, down_weight):
@@ -69,9 +78,239 @@
     return mixed_out.astype(jnp.bfloat16)
 
 
+def flip(index, mask, count):
+    total, bit = 0, 1
+    while bit < count:
+        digit = (index // bit) % 2
+        total = total + bit * ((1 - digit) if mask & bit else digit)
+        bit *= 2
+    return total
+
+
+def fused(
+    parts, blks, subs, tokens, ids, levels, gate_hbm, up_hbm, down_hbm, out,
+    taken, picked, rows, gate, up, down, gate_sum, up_sum, hidden, made, home, mixed, landed,
+    load_sem, tok_send, tok_recv, pick_send, pick_recv, made_send, made_recv, mix_send, mix_recv,
+):
+    plane = parts * blks
+    part, blk, sub = lax.axis_index("parts"), lax.axis_index("blk"), lax.axis_index("sub")
+    mine = blk * parts + part
+    width = tokens.shape[1]
+    block_rows = tokens.shape[0]
+    units = hidden.shape[1]
+
+    def at(slot, depth):
+        return {"parts": slot % parts, "blk": slot // parts, "sub": depth}
+
+    quarters = [flip(sub, j, subs) for j in range(subs)]
+    peers = [flip(mine, k, plane) for k in range(plane)]
+
+    loads = []
+    for j in range(subs):
+        span = pl.ds(pl.multiple_of(quarters[j] * width, width), width)
+        loads.append(pltpu.make_async_copy(gate_hbm.at[part, span, :], gate.at[j], load_sem.at[2 * j]))
+        loads.append(pltpu.make_async_copy(up_hbm.at[part, span, :], up.at[j], load_sem.at[2 * j + 1]))
+    for i, j in enumerate(reversed(range(subs))):
+        span = pl.ds(pl.multiple_of(quarters[j] * width, width), width)
+        loads.append(pltpu.make_async_copy(down_hbm.at[part, :, span], down.at[j], load_sem.at[2 * subs + i]))
+    for load in loads[:AHEAD]:
+        load.start()
+
+    barrier = pltpu.get_barrier_semaphore()
+    for k in range(1, plane):
+        pl.semaphore_signal(barrier, inc=1, device_id=at(peers[k], sub), device_id_type=pl.DeviceIdType.MESH)
+    for j in range(1, subs):
+        pl.semaphore_signal(barrier, inc=1, device_id=at(mine, quarters[j]), device_id_type=pl.DeviceIdType.MESH)
+
+    columns = E * CAP
+    column = lax.broadcasted_iota(jnp.int32, (block_rows, columns), 1)
+    expert, place = column // CAP, column % CAP
+    first = jnp.broadcast_to(ids[:, 0:1], (block_rows, columns)) == expert
+    second = jnp.broadcast_to(ids[:, 1:2], (block_rows, columns)) == expert
+    named = jnp.where(first | second, 1.0, 0.0).astype(F32)
+    before = lax.broadcasted_iota(jnp.int32, (block_rows, block_rows), 0) > lax.broadcasted_iota(
+        jnp.int32, (block_rows, block_rows), 1
+    )
+    rank = jnp.dot(jnp.where(before, 1.0, 0.0).astype(BF16), named.astype(BF16), preferred_element_type=F32)
+    here = jnp.where(rank == place.astype(F32), named, 0.0)
+    chosen = here.astype(BF16)
+    level = levels[...].astype(F32) + 1.0
+    share = level / (level[:, 0:1] + level[:, 1:2])
+    weight = here * jnp.where(
+        first,
+        jnp.broadcast_to(share[:, 0:1], (block_rows, columns)),
+        jnp.broadcast_to(share[:, 1:2], (block_rows, columns)),
+    )
+    weight_high = weight.astype(BF16)
+    weight_low = (weight - weight_high.astype(F32)).astype(BF16)
+
+    pl.semaphore_wait(barrier, plane + subs - 2)
+
+    tok_copies = {}
+    for j in range(1, subs):
+        tok_copies[j] = pltpu.make_async_remote_copy(
+            src_ref=tokens, dst_ref=taken.at[j], send_sem=tok_send.at[j], recv_sem=tok_recv.at[j],
+            device_id=at(mine, quarters[j]), device_id_type=pl.DeviceIdType.MESH,
+        )
+        tok_copies[j].start()
+
+    def dispatch(j):
+        if j > 0:
+            tok_copies[j].wait_recv()
+        block = tokens[...] if j == 0 else taken[j]
+        sent = lax.dot_general(chosen, block, (((0,), (0,)), ((), ())), preferred_element_type=F32)
+        picked[j] = sent.astype(BF16).reshape(plane, CAP, width)
+        copies = []
+        for k in reversed(range(1, plane)):
+            copy = pltpu.make_async_remote_copy(
+                src_ref=picked.at[j, peers[k]], dst_ref=rows.at[j, mine],
+                send_sem=pick_send.at[j, k], recv_sem=pick_recv.at[j, k],
+                device_id=at(peers[k], sub), device_id_type=pl.DeviceIdType.MESH,
+            )
+            copy.start()
+            copies.append(copy)
+        rows[j, mine] = picked[j, mine]
+        return copies
+
+    pick_copies = [dispatch(j) for j in range(subs)]
+
+    started = AHEAD
+    for j in range(subs):
+        for copy in pick_copies[j]:
+            copy.wait_recv()
+        for i in (2 * j, 2 * j + 1):
+            loads[i].wait()
+            if started < len(loads):
+                loads[started].start()
+                started += 1
+
+        @pl.loop(0, units // TILE)
+        def _(step, j=j):
+            span = pl.ds(pl.multiple_of(step * TILE, TILE), TILE)
+            x = rows[j].reshape(plane * CAP, width)
+            g = jnp.dot(x, gate[j, :, span], preferred_element_type=F32)
+            u = jnp.dot(x, up[j, :, span], preferred_element_type=F32)
+            if j > 0:
+                g = g + gate_sum[:, span]
+                u = u + up_sum[:, span]
+            if j < subs - 1:
+                gate_sum[:, span] = g
+                up_sum[:, span] = u
+            else:
+                hidden[:, span] = (g / (1.0 + jnp.exp(-g)) * u).astype(BF16)
+
+    made_copies = {}
+    mix_copies = {}
+
+    def ship(j):
+        copies = []
+        for k in reversed(range(1, plane)):
+            copy = pltpu.make_async_remote_copy(
+                src_ref=made.at[j, peers[k]], dst_ref=home.at[j, mine],
+                send_sem=made_send.at[j, k], recv_sem=made_recv.at[j, k],
+                device_id=at(peers[k], sub), device_id_type=pl.DeviceIdType.MESH,
+            )
+            copy.start()
+            copies.append(copy)
+        home[j, mine] = made[j, mine]
+        made_copies[j] = copies
+
+    def combine(j):
+        for copy in made_copies[j]:
+            copy.wait_recv()
+        block = home[j].reshape(plane * CAP, width)
+        return jnp.dot(weight_high, block, preferred_element_type=F32) + jnp.dot(
+            weight_low, block, preferred_element_type=F32
+        )
+
+    for i, j in enumerate(reversed(range(subs))):
+        loads[2 * subs + i].wait()
+        if started < len(loads):
+            loads[started].start()
+            started += 1
+
+        @pl.loop(0, width // TILE)
+        def _(step, j=j):
+            span = pl.ds(pl.multiple_of(step * TILE, TILE), TILE)
+            y = jnp.dot(hidden[...], down[j, :, span], preferred_element_type=F32)
+            made[j, :, :, span] = y.astype(BF16).reshape(plane, CAP, TILE)
+
+        ship(j)
+
+    for j in reversed(range(1, subs)):
+        mixed[j] = combine(j).astype(BF16)
+        mix_copies[j] = pltpu.make_async_remote_copy(
+            src_ref=mixed.at[j], dst_ref=landed.at[j], send_sem=mix_send.at[j], recv_sem=mix_recv.at[j],
+            device_id=at(mine, quarters[j]), device_id_type=pl.DeviceIdType.MESH,
+        )
+        mix_copies[j].start()
+    total = combine(0)
+    for j in reversed(range(1, subs)):
+        mix_copies[j].wait_recv()
+        total = total + landed[j].astype(F32)
+    out[...] = total.astype(BF16)
+
+    for j in range(1, subs):
+        tok_copies[j].wait_send()
+        mix_copies[j].wait_send()
+    for j in range(subs):
+        for copy in pick_copies[j] + made_copies[j]:
+            copy.wait_send()
+
+
+def shared_shards(parts, blks, subs, tokens, expert_ids, gate_level, gate_weight, up_weight, down_weight):
+    block_rows, width = tokens.shape
+    plane = parts * blks
+    units = gate_weight.shape[2]
+    vmem = pl.BlockSpec(memory_space=pltpu.VMEM)
+    hbm = pl.BlockSpec(memory_space=pl.ANY)
+    dma = pltpu.SemaphoreType.DMA
+    return pl.pallas_call(
+        functools.partial(fused, parts, blks, subs),
+        out_shape=jax.ShapeDtypeStruct((block_rows, width), BF16),
+        in_specs=[vmem, vmem, vmem, hbm, hbm, hbm],
+        out_specs=vmem,
+        scratch_shapes=[
+            pltpu.VMEM((subs, block_rows, width), BF16),
+            pltpu.VMEM((subs, plane, CAP, width), BF16),
+            pltpu.VMEM((subs, plane, CAP, width), BF16),
+            pltpu.VMEM((subs, width, units), BF16),
+            pltpu.VMEM((subs, width, units), BF16),
+            pltpu.VMEM((subs, units, width), BF16),
+            pltpu.VMEM((plane * CAP, units), F32),
+            pltpu.VMEM((plane * CAP, units), F32),
+            pltpu.VMEM((plane * CAP, units), BF16),
+            pltpu.VMEM((subs, plane, CAP, width), BF16),
+            pltpu.VMEM((subs, plane, CAP, width), BF16),
+            pltpu.VMEM((subs, block_rows, width), BF16),
+            pltpu.VMEM((subs, block_rows, width), BF16),
+            dma((3 * subs,)),
+            dma((subs,)), dma((subs,)),
+            dma((subs, plane)), dma((subs, plane)),
+            dma((subs, plane)), dma((subs, plane)),
+            dma((subs,)), dma((subs,)),
+        ],
+        compiler_params=pltpu.CompilerParams(
+            collective_id=0, has_side_effects=True, vmem_limit_bytes=67043328
+        ),
+    )(tokens, expert_ids, gate_level, gate_weight, up_weight, down_weight)
+
+
+def routed(parts, blks, subs, tokens, expert_ids, gate_level, gate_weight, up_weight, down_weight):
+    plane = parts * blks
+    width = tokens.shape[1]
+    units = gate_weight.shape[2]
+    fits = gate_weight.shape[0] == parts and plane == E and plane & (plane - 1) == 0
+    fits = fits and subs & (subs - 1) == 0 and width % TILE == 0 and units % TILE == 0
+    fits = fits and tokens.shape[0] == 2 * CAP
+    arrays = (tokens, expert_ids, gate_level, gate_weight, up_weight, down_weight)
+    return shared_shards(parts, blks, subs, *arrays) if fits else shards(*arrays)
+
+
 def solution(mesh):
+    sizes = (mesh.shape["parts"], mesh.shape["blk"], mesh.shape["sub"])
     return jax.shard_map(
-        shards,
+        functools.partial(routed, *sizes),
         mesh=mesh,
         in_specs=(
             P(("parts", "blk"), "sub"),

time: 131 us -> 44 us (0.34)
  matrix products: 43 us -> 0 us
  Pallas kernels: 0 us -> 39.5 us
  blocking collectives: 34 us -> 0 us
  waiting for transfers between devices: 32.1 us -> 0 us
  between operations: 13.5 us -> 0.01 us
  starting transfers between devices: 3.41 us -> 0 us
  other arithmetic: 1.52 us -> 0 us
    dot_general x5 -> x0, matrix products: 43 us -> none  [the longest x1 14.7 us: shards(): jnp.einsum('nrf,nfd->nrd', hidden, down_weight, preferred_element_type=jn...]
    pallas_call x0 -> x1, Pallas kernels: none -> 39.5 us  [shared_shards(): pl.pallas_call(functools.partial(fused, parts, blks, subs), out_shape=jax...]
    all_to_all x1 -> x0, blocking collectives: 34 us -> none  [shards(): lax.all_to_all(copies, ('blk', 'sub'), split_axis=0, concat_axis=0, tiled...]
    reduce_scatter x1 -> x0, waiting for transfers between devices: 26.2 us -> none  [shards(): lax.psum_scatter(full_out.astype(jnp.bfloat16), 'sub', scatter_dimension=...]
    all_to_all x1 -> x0, waiting for transfers between devices: 5.87 us -> none  [shards(): lax.all_to_all(local_out, 'blk', split_axis=1, concat_axis=0, tiled=True)]
    all_to_all x1 -> x0, starting transfers between devices: 3.4 us -> none  [shards(): lax.all_to_all(local_out, 'blk', split_axis=1, concat_axis=0, tiled=True)]
    unnamed x5 -> x3, local copies, waits for them, and re-layouts: 0.8 us -> 4.19 us
    reduce_scatter x1 -> x0, local copies, waits for them, and re-layouts: 1.91 us -> none  [shards(): lax.psum_scatter(full_out.astype(jnp.bfloat16), 'sub', scatter_dimension=...]
  transfers between devices with their start and end apart: 2 -> 0, of which waited for: 2 -> 0; matrix products, arithmetic and copies ran while one was open for 0% -> 0% of each run, Pallas kernels for 0% -> 0%
where the time goes in v1:
time: 44 us; the launch traced here: 43.7 us
  Pallas kernels  39.5 us (90%)
  local copies, waits for them, and re-layouts  4.19 us (10%)
    pallas_call x1, Pallas kernels, shared_shards(): pl.pallas_call(functools.partial(fused, parts, blks, subs), out_shape=jax...  39.5 us
    unnamed x3, local copies, waits for them, and re-layouts  4.19 us

profile of v1, /device:TPU:0, one launch (start us, length us, event | category | flops | bytes accessed | tf_op | source)
XLA Modules:
  0.0 43.7 jit_solution(13353335616628207196)
XLA Ops:
  0.0 1.4 %copy.7.ids = s32[32,2]{1,0:T(8,128)} copy(s32[32,2]{0,1:T(2,128)} %param.7) | data formatting | bytes 512 | tf_op args[1]
  1.4 1.4 %copy.8.levels = s32[32,2]{1,0:T(8,128)} copy(s32[32,2]{0,1:T(2,128)} %param.8) | data formatting | bytes 512 | tf_op args[2]
  2.7 39.5 %shard_map.64 = bf16[32,1024]{1,0:T(8,128)(2,1)} custom-call(bf16[32,1024]{1,0:T(8,128)(2,1)} %tokens.1, s32[32,2]{1,0:T(8,128)} %copy.7.ids, s32[32,2]{1,0:T(8,128)} %copy.8.levels, bf16[2,4096,2048]{2,1,0:T(8,128)(2,1)} %gate_hbm.1, bf16[2,4096,2048]{2,1,0:T(8,128)(2,1)} %up_hbm.1, bf16[2,2048,4096]{2,1,0:T(8,128)(2,1)} %down_hbm.1), custom_call_target="tpu_custom_call" | custom-call | tf_op jit(solution)/shard_map/pallas_call | solution.py:268
  42.3 1.5 %copy.10 = bf16[32,1024]{1,0:T(8,128)(2,1)} copy(bf16[32,1024]{1,0:T(8,128)(2,1)} %shard_map.64) | data formatting | bytes 131072

commit v2 on v1

--- a/solution.py
+++ b/solution.py
@@ -13,7 +13,7 @@
 CAP = 16
 BF16 = jnp.bfloat16
 F32 = jnp.float32
-TILE = 512
+TILE = 1024
 AHEAD = 6
 
 
@@ -88,22 +88,31 @@
 
 
 def fused(
-    parts, blks, subs, tokens, ids, levels, gate_hbm, up_hbm, down_hbm, out,
+    parts, blks, subs, tokens_hbm, ids, levels, gate_hbm, up_hbm, down_hbm, out,
     taken, picked, rows, gate, up, down, gate_sum, up_sum, hidden, made, home, mixed, landed,
-    load_sem, tok_send, tok_recv, pick_send, pick_recv, made_send, made_recv, mix_send, mix_recv,
+    load_sem, own_sem, tok_send, tok_recv, pick_send, pick_recv, made_send, made_recv, mix_send, mix_recv, relay_send, relay_recv,
 ):
     plane = parts * blks
     part, blk, sub = lax.axis_index("parts"), lax.axis_index("blk"), lax.axis_index("sub")
     mine = blk * parts + part
-    width = tokens.shape[1]
-    block_rows = tokens.shape[0]
+    block_rows, width = tokens_hbm.shape
     units = hidden.shape[1]
 
     def at(slot, depth):
         return {"parts": slot % parts, "blk": slot // parts, "sub": depth}
 
+    near = width // 4
+    far = pl.ds(near, width - near)
     quarters = [flip(sub, j, subs) for j in range(subs)]
     peers = [flip(mine, k, plane) for k in range(plane)]
+
+    own = pltpu.make_async_copy(tokens_hbm, taken.at[0], own_sem)
+    own.start()
+    barrier = pltpu.get_barrier_semaphore()
+    for k in range(1, plane):
+        pl.semaphore_signal(barrier, inc=1, device_id=at(peers[k], sub), device_id_type=pl.DeviceIdType.MESH)
+    for j in range(1, subs):
+        pl.semaphore_signal(barrier, inc=1, device_id=at(mine, quarters[j]), device_id_type=pl.DeviceIdType.MESH)
 
     loads = []
     for j in range(subs):
@@ -116,84 +125,102 @@
     for load in loads[:AHEAD]:
         load.start()
 
-    barrier = pltpu.get_barrier_semaphore()
-    for k in range(1, plane):
-        pl.semaphore_signal(barrier, inc=1, device_id=at(peers[k], sub), device_id_type=pl.DeviceIdType.MESH)
-    for j in range(1, subs):
-        pl.semaphore_signal(barrier, inc=1, device_id=at(mine, quarters[j]), device_id_type=pl.DeviceIdType.MESH)
-
-    columns = E * CAP
-    column = lax.broadcasted_iota(jnp.int32, (block_rows, columns), 1)
-    expert, place = column // CAP, column % CAP
-    first = jnp.broadcast_to(ids[:, 0:1], (block_rows, columns)) == expert
-    second = jnp.broadcast_to(ids[:, 1:2], (block_rows, columns)) == expert
+    lines = E * CAP
+    line = lax.broadcasted_iota(jnp.int32, (lines, block_rows), 0)
+    expert, place = line // CAP, line % CAP
+    first = jnp.broadcast_to(ids[0:1, :], (lines, block_rows)) == expert
+    second = jnp.broadcast_to(ids[1:2, :], (lines, block_rows)) == expert
     named = jnp.where(first | second, 1.0, 0.0).astype(F32)
-    before = lax.broadcasted_iota(jnp.int32, (block_rows, block_rows), 0) > lax.broadcasted_iota(
+    before = lax.broadcasted_iota(jnp.int32, (block_rows, block_rows), 0) < lax.broadcasted_iota(
         jnp.int32, (block_rows, block_rows), 1
     )
-    rank = jnp.dot(jnp.where(before, 1.0, 0.0).astype(BF16), named.astype(BF16), preferred_element_type=F32)
+    rank = jnp.dot(named.astype(BF16), jnp.where(before, 1.0, 0.0).astype(BF16), preferred_element_type=F32)
     here = jnp.where(rank == place.astype(F32), named, 0.0)
     chosen = here.astype(BF16)
-    level = levels[...].astype(F32) + 1.0
-    share = level / (level[:, 0:1] + level[:, 1:2])
-    weight = here * jnp.where(
-        first,
-        jnp.broadcast_to(share[:, 0:1], (block_rows, columns)),
-        jnp.broadcast_to(share[:, 1:2], (block_rows, columns)),
-    )
-    weight_high = weight.astype(BF16)
-    weight_low = (weight - weight_high.astype(F32)).astype(BF16)
-
+
+    own.wait()
     pl.semaphore_wait(barrier, plane + subs - 2)
 
     tok_copies = {}
     for j in range(1, subs):
         tok_copies[j] = pltpu.make_async_remote_copy(
-            src_ref=tokens, dst_ref=taken.at[j], send_sem=tok_send.at[j], recv_sem=tok_recv.at[j],
+            src_ref=taken.at[0, :, far], dst_ref=taken.at[j, :, far], send_sem=tok_send.at[j], recv_sem=tok_recv.at[j],
             device_id=at(mine, quarters[j]), device_id_type=pl.DeviceIdType.MESH,
         )
         tok_copies[j].start()
 
-    def dispatch(j):
-        if j > 0:
+    half = width // 2
+    spans_in = [(0, 0, near), (0, near, width - near)]
+    spans_in += [(j, near, width - near) for j in range(1, subs - 1)]
+    spans_in += [(subs - 1, near, half - near), (subs - 1, half, half)]
+    spans_out = [(subs - 1, 0, half), (subs - 1, half, half)] + [(j, 0, width) for j in reversed(range(subs - 1))]
+
+    def dispatch(n, j, start, size):
+        span = pl.ds(start, size)
+        if j > 0 and start == near:
             tok_copies[j].wait_recv()
-        block = tokens[...] if j == 0 else taken[j]
-        sent = lax.dot_general(chosen, block, (((0,), (0,)), ((), ())), preferred_element_type=F32)
-        picked[j] = sent.astype(BF16).reshape(plane, CAP, width)
+        sent = jnp.dot(chosen, taken[j, :, span], preferred_element_type=F32)
+        picked[j, :, :, span] = sent.astype(BF16).reshape(plane, CAP, size)
         copies = []
         for k in reversed(range(1, plane)):
             copy = pltpu.make_async_remote_copy(
-                src_ref=picked.at[j, peers[k]], dst_ref=rows.at[j, mine],
-                send_sem=pick_send.at[j, k], recv_sem=pick_recv.at[j, k],
+                src_ref=picked.at[j, peers[k], :, span], dst_ref=rows.at[j, mine, :, span],
+                send_sem=pick_send.at[n, k], recv_sem=pick_recv.at[n, k],
                 device_id=at(peers[k], sub), device_id_type=pl.DeviceIdType.MESH,
             )
             copy.start()
             copies.append(copy)
-        rows[j, mine] = picked[j, mine]
+        rows[j, mine, :, span] = picked[j, mine, :, span]
         return copies
 
-    pick_copies = [dispatch(j) for j in range(subs)]
+    pick_copies = [dispatch(n, *piece) for n, piece in enumerate(spans_in[:2])]
+    for copy in pick_copies[0]:
+        copy.wait_recv()
+    relays = {}
+    for j in range(1, subs):
+        relays[j] = pltpu.make_async_remote_copy(
+            src_ref=rows.at[0, :, :, pl.ds(0, near)], dst_ref=rows.at[j, :, :, pl.ds(0, near)],
+            send_sem=relay_send.at[j], recv_sem=relay_recv.at[j],
+            device_id=at(mine, quarters[j]), device_id_type=pl.DeviceIdType.MESH,
+        )
+        relays[j].start()
+    pick_copies += [dispatch(n + 2, *piece) for n, piece in enumerate(spans_in[2:])]
+
+    level = levels[...].astype(F32) + 1.0
+    share = level / (level[0:1, :] + level[1:2, :])
+    weight = here * jnp.where(
+        first,
+        jnp.broadcast_to(share[0:1, :], (lines, block_rows)),
+        jnp.broadcast_to(share[1:2, :], (lines, block_rows)),
+    )
+    weight = weight.T
+    weight_high = weight.astype(BF16)
+    weight_low = (weight - weight_high.astype(F32)).astype(BF16)
 
     started = AHEAD
-    for j in range(subs):
-        for copy in pick_copies[j]:
+    spans_used = [(j, 0, width) for j in range(subs - 1)] + [(subs - 1, 0, half), (subs - 1, half, half)]
+    for n, (j, start, size) in enumerate(spans_used):
+        if start == 0:
+            if j > 0:
+                relays[j].wait_recv()
+            for i in (2 * j, 2 * j + 1):
+                loads[i].wait()
+                if started < len(loads):
+                    loads[started].start()
+                    started += 1
+        for copy in pick_copies[n + 1]:
             copy.wait_recv()
-        for i in (2 * j, 2 * j + 1):
-            loads[i].wait()
-            if started < len(loads):
-                loads[started].start()
-                started += 1
 
         @pl.loop(0, units // TILE)
-        def _(step, j=j):
+        def _(step, n=n, j=j, depth=pl.ds(start, size)):
             span = pl.ds(pl.multiple_of(step * TILE, TILE), TILE)
-            x = rows[j].reshape(plane * CAP, width)
-            g = jnp.dot(x, gate[j, :, span], preferred_element_type=F32)
-            u = jnp.dot(x, up[j, :, span], preferred_element_type=F32)
-            if j > 0:
+            x = rows[j, :, :, depth].reshape(plane * CAP, depth.size)
+            g = jnp.dot(x, gate[j, depth, span], preferred_element_type=F32)
+            u = jnp.dot(x, up[j, depth, span], preferred_element_type=F32)
+            if n > 0:
                 g = g + gate_sum[:, span]
                 u = u + up_sum[:, span]
-            if j < subs - 1:
+            if n < len(spans_used) - 1:
                 gate_sum[:, span] = g
                 up_sum[:, span] = u
             else:
@@ -202,18 +229,18 @@
     made_copies = {}
     mix_copies = {}
 
-    def ship(j):
+    def ship(n, j, span):
         copies = []
         for k in reversed(range(1, plane)):
             copy = pltpu.make_async_remote_copy(
-                src_ref=made.at[j, peers[k]], dst_ref=home.at[j, mine],
-                send_sem=made_send.at[j, k], recv_sem=made_recv.at[j, k],
+                src_ref=made.at[j, peers[k], :, span], dst_ref=home.at[j, mine, :, span],
+                send_sem=made_send.at[n, k], recv_sem=made_recv.at[n, k],
                 device_id=at(peers[k], sub), device_id_type=pl.DeviceIdType.MESH,
             )
             copy.start()
             copies.append(copy)
-        home[j, mine] = made[j, mine]
-        made_copies[j] = copies
+        home[j, mine, :, span] = made[j, mine, :, span]
+        made_copies.setdefault(j, []).extend(copies)
 
     def combine(j):
         for copy in made_copies[j]:
@@ -223,19 +250,21 @@
             weight_low, block, preferred_element_type=F32
         )
 
-    for i, j in enumerate(reversed(range(subs))):
-        loads[2 * subs + i].wait()
-        if started < len(loads):
-            loads[started].start()
-            started += 1
-
-        @pl.loop(0, width // TILE)
-        def _(step, j=j):
-            span = pl.ds(pl.multiple_of(step * TILE, TILE), TILE)
+    for n, (j, start, size) in enumerate(spans_out):
+        if start == 0:
+            loads[2 * subs + subs - 1 - j].wait()
+            if started < len(loads):
+                loads[started].start()
+                started += 1
+        step = size // 2
+
+        @pl.loop(0, 2)
+        def _(turn, j=j, start=start, step=step):
+            span = pl.ds(pl.multiple_of(start + turn * step, step), step)
             y = jnp.dot(hidden[...], down[j, :, span], preferred_element_type=F32)
-            made[j, :, :, span] = y.astype(BF16).reshape(plane, CAP, TILE)
-
-        ship(j)
+            made[j, :, :, span] = y.astype(BF16).reshape(plane, CAP, step)
+
+        ship(n, j, pl.ds(start, size))
 
     for j in reversed(range(1, subs)):
         mixed[j] = combine(j).astype(BF16)
@@ -252,9 +281,10 @@
 
     for j in range(1, subs):
         tok_copies[j].wait_send()
+        relays[j].wait_send()
         mix_copies[j].wait_send()
-    for j in range(subs):
-        for copy in pick_copies[j] + made_copies[j]:
+    for copies in pick_copies + list(made_copies.values()):
+        for copy in copies:
             copy.wait_send()
 
 
@@ -268,7 +298,7 @@
     return pl.pallas_call(
         functools.partial(fused, parts, blks, subs),
         out_shape=jax.ShapeDtypeStruct((block_rows, width), BF16),
-        in_specs=[vmem, vmem, vmem, hbm, hbm, hbm],
+        in_specs=[hbm, vmem, vmem, hbm, hbm, hbm],
         out_specs=vmem,
         scratch_shapes=[
             pltpu.VMEM((subs, block_rows, width), BF16),
@@ -284,16 +314,17 @@
             pltpu.VMEM((subs, plane, CAP, width), BF16),
             pltpu.VMEM((subs, block_rows, width), BF16),
             pltpu.VMEM((subs, block_rows, width), BF16),
-            dma((3 * subs,)),
+            dma((3 * subs,)), pltpu.SemaphoreType.DMA,
             dma((subs,)), dma((subs,)),
-            dma((subs, plane)), dma((subs, plane)),
-            dma((subs, plane)), dma((subs, plane)),
+            dma((subs + 2, plane)), dma((subs + 2, plane)),
+            dma((subs + 1, plane)), dma((subs + 1, plane)),
+            dma((subs,)), dma((subs,)),
             dma((subs,)), dma((subs,)),
         ],
         compiler_params=pltpu.CompilerParams(
             collective_id=0, has_side_effects=True, vmem_limit_bytes=67043328
         ),
-    )(tokens, expert_ids, gate_level, gate_weight, up_weight, down_weight)
+    )(tokens, expert_ids.T, gate_level.T, gate_weight, up_weight, down_weight)
 
 
 def routed(parts, blks, subs, tokens, expert_ids, gate_level, gate_weight, up_weight, down_weight):

time: 44 us -> 39.7 us (0.902)
  local copies, waits for them, and re-layouts: 4.19 us -> 1.47 us
  Pallas kernels: 39.5 us -> 38.1 us
    unnamed x3 -> x1, local copies, waits for them, and re-layouts: 4.19 us -> 1.47 us
    pallas_call x1, Pallas kernels: 39.5 us -> 38.1 us  [shared_shards(): pl.pallas_call(functools.partial(fused, parts, blks, subs), out_shape=jax...]
where the time goes in v2:
time: 39.7 us; the launch traced here: 39.6 us
  Pallas kernels  38.1 us (96%)
  local copies, waits for them, and re-layouts  1.47 us (4%)
    pallas_call x1, Pallas kernels, shared_shards(): pl.pallas_call(functools.partial(fused, parts, blks, subs), out_shape=jax...  38.1 us
    unnamed x1, local copies, waits for them, and re-layouts  1.47 us

profile of v2, /device:TPU:0, one launch (start us, length us, event | category | flops | bytes accessed | tf_op | source)
XLA Modules:
  0.0 39.6 jit_solution(17642359046459568418)
XLA Ops:
  0.0 38.1 %shard_map.64 = bf16[32,1024]{1,0:T(8,128)(2,1)} custom-call(bf16[32,1024]{1,0:T(8,128)(2,1)} %tokens_hbm.1, s32[2,32]{1,0:T(2,128)} %bitcast.2, s32[2,32]{1,0:T(2,128)} %bitcast.3, bf16[2,4096,2048]{2,1,0:T(8,128)(2,1)} %gate_hbm.1, bf16[2,4096,2048]{2,1,0:T(8,128)(2,1)} %up_hbm.1, bf16[2,2048,4096]{2,1,0:T(8,128)(2,1)} %down_hbm.1), custom_call_target="tpu_custom_call" | custom-call | tf_op jit(solution)/shard_map/pallas_call | solution.py:298
  38.1 1.5 %copy.8 = bf16[32,1024]{1,0:T(8,128)(2,1)} copy(bf16[32,1024]{1,0:T(8,128)(2,1)} %shard_map.64) | data formatting | bytes 131072
